TPU v7x, 32 devices: a whole 2x2x4 slice. The times are simulated.
32 devices in a mesh: groups: 2 (over y), tmpl: 8 (over z, x), det: 2 (over core).
Axes of the slice: x: 2, y: 2, z: 4, core: 2. Of those that a mesh axis runs over, the one named last changes fastest.
Arguments:
- basis_series: bfloat16 [3, 128, 32768], P(None, None, ('groups', 'tmpl', 'det')), parts along dimension 2, may hold values from -6 to 6
- reconstruction: bfloat16 [3, 256, 2, 128], P(None, ('groups', 'tmpl')), parts along dimension 1, may hold values from -0.5 to 0.5
- offsets: int32 [6], P('groups'), parts along dimension 0, may hold values from 1024 to 16383
Outputs:
- window_peaks: float32 [128, 256], P(None, ('groups', 'tmpl', 'det')), parts along dimension 1
There are 2 independent parts, one for each index of `groups`. A program takes and returns all parts, laid end to end along the dimension named above; each array names one. Nothing has to cross between parts.
Inputs may be any that keep to these rules, and one draw needn't show every extreme that they name: `offsets`: slides are applied circularly over the segment's 16384 samples.
All inputs are finite; a program needn't handle non-finite values.
Results may differ from a plain program's by a relative error of at most 0.0003.
Values may be sent and summed in bfloat16 or wider, within the bound.
A program may use at most 64 MiB of HBM per device.

v0:
```python
import functools
import math

import jax
import jax.numpy as jnp
from jax import lax
from jax.experimental import pallas as pl
from jax.experimental.pallas import tpu as pltpu
from jax.sharding import PartitionSpec as P

WIN = 128
SLIDE_BLOCKS = 16
MESH = pl.DeviceIdType.MESH
TINY = 1e-18
CODE = jnp.int16
SPAN = 30
STEPS = 1092
TOP = 15


def coded(power):
    log = jnp.log(jnp.maximum(power, 2.0 ** (TOP - 2 * SPAN))) * (STEPS / math.log(2.0))
    return jnp.round(log - (TOP - SPAN) * STEPS).astype(jnp.int32).astype(CODE)


def decoded(code):
    code = code.astype(jnp.int32).astype(jnp.float32)
    power = jnp.exp2(code * (1.0 / STEPS) + (TOP - SPAN))
    return jnp.where(code <= -SPAN * STEPS, 0.0, power)


def partner(chip, chips, k, sign):
    half = chips // 2
    near = k // half
    turn = k - near * half + near
    side = lax.rem(lax.div(chip, half) + 1 - near, 2)
    return side * half + lax.rem(lax.rem(chip, half) + half + sign * turn, half)


def kernel(
    chips, cores,
    off_hbm, basis_hbm, bank_hbm, out_ref,
    off_ref, basis_ref, bank_ref, bank_all, top_all, stage, recv, dec, peaks, final,
    load, bank_s, bank_r, pass_s, top_s, top_r, pow_s, pow_r, peak_s, peak_r,
):
    dets, basis, block = basis_ref.shape
    rows2 = bank_ref.shape[1] // cores
    rows = rows2 // 2
    half = block // 2
    wins = block // WIN
    count = chips * cores
    total = count * wins
    per_row = WIN // rows
    chip, core = lax.axis_index("tmpl"), lax.axis_index("det")
    me = chip * cores + core

    load_bank = pltpu.make_async_copy(bank_hbm, bank_ref, load.at[0])
    load_basis = pltpu.make_async_copy(basis_hbm, basis_ref, load.at[1])
    load_off = pltpu.make_async_copy(off_hbm, off_ref, load.at[2])
    load_bank.start()
    load_basis.start()
    load_off.start()

    def dev(j, c):
        return {"tmpl": j, "det": c}

    def over_chips(fn, sign=1, short=True):
        if short and chips <= 8:
            for k in range(chips - 1):
                fn(partner(chip, chips, k, sign))
            return

        @pl.loop(0, chips - 1)
        def _(k):
            fn(partner(chip, chips, k, sign))

    def over_peers(fn, sign=1):
        for d in range(cores):
            over_chips(lambda j: fn(j, lax.rem(core + d, cores)), sign)
        for d in range(1, cores):
            fn(chip, lax.rem(core + d, cores))

    barrier = pltpu.get_barrier_semaphore()
    over_peers(lambda j, c: pl.semaphore_signal(barrier, inc=1, device_id=dev(j, c), device_id_type=MESH))

    mine = pl.ds(pl.multiple_of(core * rows2, rows2), rows2)

    def bank_copy(j, src):
        return pltpu.make_async_remote_copy(
            src_ref=bank_ref.at[:, mine], dst_ref=bank_all.at[src],
            send_sem=bank_s.at[j], recv_sem=bank_r.at[src],
            device_id=dev(j, core), device_id_type=MESH)

    def pass_copy(src, c):
        return pltpu.make_async_remote_copy(
            src_ref=bank_all.at[src], dst_ref=bank_all.at[src],
            send_sem=pass_s.at[lax.div(src, cores) * cores + c], recv_sem=bank_r.at[src],
            device_id=dev(chip, c), device_id_type=MESH)

    def top_copy(j, c, src):
        return pltpu.make_async_remote_copy(
            src_ref=top_all.at[src], dst_ref=top_all.at[src],
            send_sem=top_s.at[j * cores + c], recv_sem=top_r.at[src],
            device_id=dev(j, c), device_id_type=MESH)

    def pow_copy(j, c, src):
        return pltpu.make_async_remote_copy(
            src_ref=stage.at[j * cores + c], dst_ref=recv.at[src],
            send_sem=pow_s.at[j * cores + c], recv_sem=pow_r.at[src],
            device_id=dev(j, c), device_id_type=MESH)

    def peak_copy(j, c, src):
        return pltpu.make_async_remote_copy(
            src_ref=peaks.at[(j * cores + c) * wins // per_row], dst_ref=final.at[src],
            send_sem=peak_s.at[j * cores + c], recv_sem=peak_r.at[src],
            device_id=dev(j, c), device_id_type=MESH)

    r = lax.broadcasted_iota(jnp.int32, (dets * rows2, dets * rows2), 0)
    i = lax.broadcasted_iota(jnp.int32, (dets * rows2, dets * rows2), 1)
    d_of = lax.div(r, rows2)
    k_of = lax.rem(lax.div(r, rows), 2)
    m_of = lax.rem(r, rows)
    perm = (i == d_of * rows2 + m_of * 2 + k_of).astype(jnp.float32).astype(jnp.bfloat16)

    def largest(x):
        x = jnp.max(jnp.abs(x).astype(jnp.float32), axis=0)
        return jnp.max(jnp.max(x, axis=0, keepdims=True), axis=1, keepdims=True)

    load_bank.wait()
    load_basis.wait()
    load_off.wait()
    top = largest(basis_ref[...])
    top_all[me] = jnp.broadcast_to(top, (1, WIN))
    own_max = largest(bank_ref[:, mine])

    def power_for(to, bank):
        a = jnp.maximum(largest(bank) * top, TINY)
        inv = 1.0 / (a * a)
        w = jnp.dot(perm, bank.reshape(dets * rows2, basis), preferred_element_type=jnp.float32).astype(jnp.bfloat16)
        for d in range(dets):
            f = jnp.dot(w[d * rows2:(d + 1) * rows2], basis_ref[d], preferred_element_type=jnp.float32)
            f = f * f
            p = (f[:rows] + f[rows:]) * inv
            stage[to, d] = coded(jnp.concatenate([p[:, :half], p[:, half:]], axis=0))

    for c in range(cores):
        power_for(chip * cores + c, bank_ref[:, c * rows2:(c + 1) * rows2])

    pl.semaphore_wait(barrier, count - 1)
    over_chips(lambda j: bank_copy(j, me).start())
    over_peers(lambda j, c: top_copy(j, c, me).start())
    for d in range(1, cores):
        pow_copy(chip, lax.rem(core + d, cores), me).start()

    def direct(j):
        src = j * cores + core
        bank_copy(chip, src).wait_recv()
        for d in range(1, cores):
            pass_copy(src, lax.rem(core + d, cores)).start()
        power_for(src, bank_all[src])
        pow_copy(j, core, me).start()

    over_chips(direct, -1, short=False)

    for d in range(1, cores):
        other = lax.rem(core + d, cores)

        def passed_on(j):
            src = j * cores + other
            bank_copy(chip, src).wait_recv()
            power_for(src, bank_all[src])
            pow_copy(j, other, me).start()

        over_chips(passed_on, -1, short=False)

    rest = [lax.rem(off_ref[d], WIN) for d in range(dets)]
    shifts = [lax.div(off_ref[d], WIN) for d in range(dets)]

    def decode(src, value):
        a = jnp.maximum(top_all[src] * own_max, TINY)
        scale = a * a
        for d in range(dets):
            x = decoded(value(d))
            tiles = []
            for v in range(wins):
                h, q = divmod(v, wins // 2)
                tile = x[h * rows:(h + 1) * rows, q * WIN:(q + 1) * WIN] * scale
                tile = pltpu.roll(tile, WIN - rest[d], 1)
                dec[d, src * wins + v] = tile
                tiles.append(tile)

            @pl.when(src < SLIDE_BLOCKS)
            def _():
                for v in range(wins):
                    dec[d, (count + src) * wins + v] = tiles[v]

    decode(me, lambda d: stage[me, d])

    def take(j, c):
        src = j * cores + c
        top_copy(chip, core, src).wait_recv()
        pow_copy(chip, core, src).wait_recv()
        decode(src, lambda d: recv[src, d])

    for d in range(1, cores):
        take(chip, lax.rem(core + d, cores))
    for d in range(cores):
        over_chips(lambda j: take(j, lax.rem(core + d, cores)), short=False)

    lane = lax.broadcasted_iota(jnp.int32, (per_row, rows, WIN), 2)

    @pl.loop(0, total // per_row, unroll=8)
    def _(g):
        power = None
        for d in range(dets):
            tiles = dec[d, pl.ds(g * per_row + shifts[d], per_row + 1)]
            x = jnp.where(lane < WIN - rest[d], tiles[:per_row], tiles[1:])
            power = x if power is None else power + x
        turned = power.reshape(per_row * rows, WIN).T
        peaks[g] = jnp.sqrt(jnp.max(turned, axis=0, keepdims=True))

    over_peers(lambda j, c: peak_copy(j, c, me).start())
    final[me] = peaks[me * wins // per_row]
    over_peers(lambda j, c: peak_copy(chip, core, j * cores + c).wait_recv(), -1)

    base = lax.rem(me * wins, per_row) * rows
    e_of = lax.broadcasted_iota(jnp.int32, (per_row, WIN), 0)
    l_of = lax.broadcasted_iota(jnp.int32, (per_row, WIN), 1)
    for g in range(count // per_row):
        x = final[g * per_row:(g + 1) * per_row].reshape(per_row, WIN)
        x = pltpu.roll(x, lax.rem(WIN - base, WIN), 1)
        x = jnp.concatenate([
            pltpu.roll(x[h:h + 8], h * rows, 1, stride=rows, stride_axis=0) for h in range(0, per_row, 8)], axis=0)
        for i in range(wins):
            y = pltpu.roll(x, (WIN - i * rows) % WIN, 1)
            y = jnp.where(lax.div(l_of, rows) == e_of, y, 0.0)
            out_ref[i:i + 1, g * WIN:(g + 1) * WIN] = jnp.sum(y, axis=0, keepdims=True)

    over_chips(lambda j: bank_copy(j, me).wait_send())

    def passed(j):
        for d in range(1, cores):
            pass_copy(j * cores + core, lax.rem(core + d, cores)).wait_send()

    over_chips(passed)

    def drain(j, c):
        top_copy(j, c, me).wait_send()
        pow_copy(j, c, me).wait_send()
        peak_copy(j, c, me).wait_send()

    over_peers(drain)


def per_device(chips, cores, basis_series, reconstruction, offsets):
    dets, basis, block = basis_series.shape
    templates = reconstruction.shape[1]
    bank = reconstruction.reshape(dets, templates * 2, basis)
    count = chips * cores
    rows = templates // cores
    wins = block // WIN
    total = count * wins
    per_row = WIN // rows
    hbm = pl.BlockSpec(memory_space=pltpu.HBM)
    out = pl.pallas_call(
        functools.partial(kernel, chips, cores),
        out_shape=jax.ShapeDtypeStruct((wins, count * rows), jnp.float32),
        in_specs=[hbm, hbm, hbm],
        out_specs=pl.BlockSpec(memory_space=pltpu.VMEM),
        scratch_shapes=[
            pltpu.SMEM(offsets.shape, offsets.dtype),
            pltpu.VMEM(basis_series.shape, basis_series.dtype),
            pltpu.VMEM(bank.shape, bank.dtype),
            pltpu.VMEM((count, dets, rows * 2, basis), jnp.bfloat16),
            pltpu.VMEM((count, 1, WIN), jnp.float32),
            pltpu.VMEM((count, dets, rows * 2, block // 2), CODE),
            pltpu.VMEM((count, dets, rows * 2, block // 2), CODE),
            pltpu.VMEM((dets, total + SLIDE_BLOCKS * wins, rows, WIN), jnp.float32),
            pltpu.VMEM((total // per_row, 1, WIN), jnp.float32),
            pltpu.VMEM((count, 1, WIN), jnp.float32),
            pltpu.SemaphoreType.DMA((3,)),
            pltpu.SemaphoreType.DMA((chips,)),
        ] + [pltpu.SemaphoreType.DMA((count,)) for _ in range(8)],
        compiler_params=pltpu.CompilerParams(
            collective_id=0, has_side_effects=True, vmem_limit_bytes=63_000_000),
    )(offsets, basis_series, bank)
    return out.T


def solution(mesh):
    chips, cores = mesh.shape["tmpl"], mesh.shape["det"]
    in_specs = (
        P(None, None, ("groups", "tmpl", "det")),
        P(None, ("groups", "tmpl"), None, None),
        P("groups"),
    )
    out_specs = P(None, ("groups", "tmpl", "det"))
    return jax.shard_map(
        functools.partial(per_device, chips, cores),
        mesh=mesh, in_specs=in_specs, out_specs=out_specs, check_vma=False,
    )
```

profile of v0, /device:TPU:0, one launch (start us, length us, event | category | flops | bytes accessed | tf_op | source)
XLA Modules:
  0.0 35.6 jit_solution(13174982901412629708)
XLA Ops:
  0.0 34.3 %shard_map.37 = f32[8,128]{1,0:T(8,128)} custom-call(s32[3]{0:T(128)} %off_hbm.1, bf16[3,128,1024]{2,1,0:T(8,128)(2,1)} %basis_hbm.1, bf16[3,32,128]{2,1,0:T(8,128)(2,1)} %bitcast.2), custom_call_target="tpu_custom_call" | custom-call | tf_op jit(solution)/shard_map/pallas_call | solution.py:265
  34.3 1.3 %copy.5 = f32[128,8]{0,1:T(8,128)} copy(f32[128,8]{0,1:T(8,128)} %bitcast.3) | data formatting | bytes 8192
where the time goes:
time: 35.8 us; the launch traced here: 35.6 us
  Pallas kernels  34.3 us (96%)
  local copies, waits for them, and re-layouts  1.28 us (4%)
    pallas_call x1, Pallas kernels, per_device(): pl.pallas_call(functools.partial(kernel, chips, cores), out_shape=jax.Sha...  34.3 us
    unnamed x1, local copies, waits for them, and re-layouts  1.28 us

commit v1 on v0

v1 whole, which is shorter than its diff:
```python
import functools
import math

import jax
import jax.numpy as jnp
from jax import lax
from jax.experimental import pallas as pl
from jax.experimental.pallas import tpu as pltpu
from jax.sharding import PartitionSpec as P

WIN = 128
SUB = 8
SLIDE_BLOCKS = 16
MESH = pl.DeviceIdType.MESH
TINY = 1e-18
CODE = jnp.int16
SPAN = 30
STEPS = 1092
TOP = 15


def coded(power):
    log = jnp.log(jnp.maximum(power, 2.0 ** (TOP - 2 * SPAN))) * (STEPS / math.log(2.0))
    return jnp.round(log - (TOP - SPAN) * STEPS).astype(jnp.int32).astype(CODE)


def decoded(code):
    code = code.astype(jnp.int32).astype(jnp.float32)
    power = jnp.exp2(code * (1.0 / STEPS) + (TOP - SPAN))
    return jnp.where(code <= -SPAN * STEPS, 0.0, power)


def kernel(
    chips, cores,
    off_hbm, basis_hbm, bank_hbm, out_ref,
    off_ref, basis_ref, bank_ref, bank_own, bank_all, stage, recv, dec, peaks, final,
    load, bank_s, fwd_s, pass_s, bank_r, pow_s, pow_r, peak_s, peak_r,
):
    dets, basis, block = basis_ref.shape
    rows2 = bank_ref.shape[1] // cores
    rows = rows2 // 2
    half = block // 2
    wins = block // WIN
    count = chips * cores
    total = count * wins
    per_row = WIN // rows
    near = chips // 2
    chip, core = lax.axis_index("tmpl"), lax.axis_index("det")
    me = chip * cores + core
    side, place = lax.div(chip, near), lax.rem(chip, near)

    load_bank = pltpu.make_async_copy(bank_hbm, bank_ref, load.at[0])
    load_basis = pltpu.make_async_copy(basis_hbm, basis_ref, load.at[1])
    load_off = pltpu.make_async_copy(off_hbm, off_ref, load.at[2])
    load_bank.start()
    load_basis.start()
    load_off.start()

    def dev(j, c):
        return {"tmpl": j, "det": c}

    def across(j):
        return lax.rem(j + near, chips)

    def close(k):
        if near & (near - 1):
            return side * near + lax.rem(place + near + k, near)
        return side * near + lax.bitwise_xor(place, jnp.int32(k))

    def facing(k):
        return close(-k if near & (near - 1) else k)

    def other_core(d):
        return lax.rem(core + d, cores)

    def over(lo, hi, fn, short=True):
        if short and hi - lo <= 8:
            for k in range(lo, hi):
                fn(k)
            return

        @pl.loop(lo, hi)
        def _(k):
            fn(k)

    def over_peers(fn):
        for d in range(1, cores):
            fn(chip, other_core(d))
        for d in range(cores):
            c = other_core(d)
            over(0, near, lambda k: fn(across(close(k)), c))
            over(1, near, lambda k: fn(close(k), c))

    barrier = pltpu.get_barrier_semaphore()
    over_peers(lambda j, c: pl.semaphore_signal(barrier, inc=1, device_id=dev(j, c), device_id_type=MESH))

    def bank_copy(j, src, sem):
        return pltpu.make_async_remote_copy(
            src_ref=bank_all.at[src], dst_ref=bank_all.at[src], send_sem=sem, recv_sem=bank_r.at[src],
            device_id=dev(j, core), device_id_type=MESH)

    def pass_copy(src, c):
        return pltpu.make_async_remote_copy(
            src_ref=bank_all.at[src], dst_ref=bank_all.at[src],
            send_sem=pass_s.at[lax.div(src, cores) * cores + c], recv_sem=bank_r.at[src],
            device_id=dev(chip, c), device_id_type=MESH)

    def pow_copy(j, c, src):
        return pltpu.make_async_remote_copy(
            src_ref=stage.at[j * cores + c], dst_ref=recv.at[src],
            send_sem=pow_s.at[j * cores + c], recv_sem=pow_r.at[src],
            device_id=dev(j, c), device_id_type=MESH)

    def peak_row(j, c):
        i = j * cores + c
        return lax.div(i, per_row) * SUB + lax.rem(SUB - lax.rem(i, SUB), SUB)

    def peak_copy(j, c, src):
        return pltpu.make_async_remote_copy(
            src_ref=peaks.at[peak_row(j, c)], dst_ref=final.at[src],
            send_sem=peak_s.at[j * cores + c], recv_sem=peak_r.at[src],
            device_id=dev(j, c), device_id_type=MESH)

    span = dets * rows2
    size = span * cores
    r = lax.broadcasted_iota(jnp.int32, (size, size), 0)
    i = lax.broadcasted_iota(jnp.int32, (size, size), 1)
    c_of = lax.div(r, span)
    d_of = lax.rem(lax.div(r, rows2), dets)
    k_of = lax.rem(lax.div(r, rows), 2)
    m_of = lax.rem(r, rows)
    perm = (i == (d_of * cores + c_of) * rows2 + m_of * 2 + k_of).astype(jnp.float32).astype(jnp.bfloat16)

    def largest(x):
        x = jnp.abs(x).astype(jnp.float32)
        x = jnp.max(x.reshape(-1, SUB, x.shape[-1]), axis=0)
        return jnp.max(jnp.max(x, axis=0, keepdims=True), axis=1, keepdims=True)

    load_bank.wait()
    sorted_bank = jnp.dot(
        perm, bank_ref[...].reshape(size, basis), preferred_element_type=jnp.float32).astype(jnp.bfloat16)
    for c in range(cores):
        bank_own[c, :span] = sorted_bank[c * span:(c + 1) * span]
    load_basis.wait()
    top = largest(basis_ref[...].reshape(dets * basis, block))
    for c in range(cores):
        own_max = largest(sorted_bank[c * span:(c + 1) * span])
        note = jnp.concatenate([jnp.broadcast_to(top, (SUB, basis)), jnp.broadcast_to(own_max, (SUB, basis))], axis=0)
        bank_own[c, span:] = note.astype(jnp.bfloat16)
    bank_all[me] = bank_own[core]

    def bank_max(bank, src):
        return bank[src, span + SUB:].astype(jnp.float32)[:1, :1]

    def powers_for(j, bank, first):
        to = across(j)
        inv = []
        for c in range(cores):
            a = jnp.maximum(bank_max(bank, first + c) * top, TINY)
            inv.append(1.0 / (a * a))
        for d in range(dets):
            w = jnp.concatenate(
                [bank[first + c, d * rows2:(d + 1) * rows2] for c in range(cores)], axis=0)
            f = jnp.dot(w, basis_ref[d], preferred_element_type=jnp.float32)
            f = f * f
            for c in range(cores):
                p = (f[c * rows2:c * rows2 + rows] + f[c * rows2 + rows:(c + 1) * rows2]) * inv[c]
                stage[to * cores + c, d] = coded(jnp.concatenate([p[:, :half], p[:, half:]], axis=0))

    def pieces(j, fn):
        for d in range(1, cores):
            fn(j * cores + other_core(d))

    powers_for(chip, bank_own, 0)
    pl.semaphore_wait(barrier, count - 1)

    bank_copy(across(chip), me, bank_s.at[0]).start()
    over(1, near, lambda k: bank_copy(facing(k), me, bank_s.at[k]).start())
    for c in range(cores):
        pow_copy(across(chip), c, me).start()
    for d in range(1, cores):
        pass_copy(me, other_core(d)).start()

    def pass_on(src):
        bank_copy(chip, src, bank_s.at[0]).wait_recv()
        for d in range(1, cores):
            pass_copy(src, other_core(d)).start()

    over(1, near, lambda k: pass_on(close(k) * cores + core))
    relay = across(chip) * cores + core
    pass_on(relay)
    over(1, near, lambda k: bank_copy(facing(k), relay, fwd_s.at[k]).start())

    def near_powers(k):
        j = close(k)
        pieces(j, lambda src: bank_copy(chip, src, bank_s.at[0]).wait_recv())
        powers_for(j, bank_all, j * cores)
        for c in range(cores):
            pow_copy(across(j), c, me).start()

    over(1, near, near_powers, short=False)

    over(1, near, lambda k: pass_on(across(close(k)) * cores + core))
    pieces(across(chip), lambda src: bank_copy(chip, src, bank_s.at[0]).wait_recv())
    powers_for(across(chip), bank_all, across(chip) * cores)
    for d in range(1, cores):
        pow_copy(chip, other_core(d), me).start()

    def far_powers(k):
        j = across(close(k))
        pieces(j, lambda src: bank_copy(chip, src, bank_s.at[0]).wait_recv())
        powers_for(j, bank_all, j * cores)
        for c in range(cores):
            pow_copy(close(k), c, me).start()

    over(1, near, far_powers, short=False)

    load_off.wait()
    rest = [lax.rem(off_ref[d], WIN) for d in range(dets)]
    shifts = [lax.div(off_ref[d], WIN) for d in range(dets)]
    owned = bank_max(bank_all, across(chip) * cores + core)

    def decode(src, value):
        a = jnp.maximum(bank_all[src, span:span + SUB].astype(jnp.float32)[:1, :1] * owned, TINY)
        scale = a * a
        for d in range(dets):
            x = decoded(value(d)) * scale
            tiles = []
            for v in range(wins):
                h, q = divmod(v, wins // 2)
                tile = x[h * rows:(h + 1) * rows, q * WIN:(q + 1) * WIN]
                tile = pltpu.roll(tile, WIN - rest[d], 1)
                dec[d, src * wins + v] = tile
                tiles.append(tile)

            @pl.when(src < SLIDE_BLOCKS)
            def _():
                for v in range(wins):
                    dec[d, (count + src) * wins + v] = tiles[v]

    decode(me, lambda d: stage[me, d])

    def take(j, c):
        src = j * cores + c
        pow_copy(chip, core, src).wait_recv()
        decode(src, lambda d: recv[src, d])

    @pl.loop(0, cores)
    def _(c):
        take(across(chip), c)

    pieces(chip, lambda src: bank_copy(chip, src, bank_s.at[0]).wait_recv())
    for d in range(1, cores):
        take(chip, other_core(d))

    def take_pair(k):
        @pl.loop(0, 2 * cores)
        def _(n):
            far = lax.div(n, cores)
            j = lax.rem(facing(k) + far * near, chips)
            take(j, lax.rem(n, cores))

    over(1, near, take_pair, short=False)

    lane = lax.broadcasted_iota(jnp.int32, (rows, WIN), 1)
    inside = [lane < WIN - rest[d] for d in range(dets)]
    bit = [lax.rem(lax.div(lane, 1 << p), 2) == 0 for p in range(7)]
    row = lax.broadcasted_iota(jnp.int32, (rows, WIN), 0)
    dest = lax.rem(SUB - row, SUB) + SUB * lax.div(lane, WIN // 2)
    index = SUB * lax.rem(dest + lax.rem(lane, SUB), per_row) + lax.rem(lax.div(lane, SUB), SUB)

    def group(g):
        base = g * WIN
        last = {}

        def tile(d, v):
            if last.get(d, (None, None))[0] != v:
                last[d] = (v, dec[d, base + shifts[d] + v])
            return last[d][1]

        def leaf(v):
            power = None
            for d in range(dets):
                lo = tile(d, v)
                x = jnp.where(inside[d], lo, tile(d, v + 1))
                power = x if power is None else power + x
            return power

        def merged(k, v):
            if k == 0:
                return leaf(v)
            p = k - 1
            a = merged(p, v)
            b = merged(p, v + (1 << p))
            s = jnp.where(bit[p], a, b)
            t = jnp.where(bit[p], b, a)
            return jnp.maximum(s, pltpu.roll(t, WIN - (1 << p), 1))

        x = jnp.sqrt(merged(7, 0))
        x = pltpu.roll(x, 0, 1, stride=SUB, stride_axis=0)
        for p in range(3):
            x = jnp.where(bit[3 + p], x, pltpu.roll(x, SUB - (1 << p), 0))
        x = jnp.take_along_axis(x, index, axis=1)
        for s in range(SUB):
            peaks[g * SUB + s] = x[s:s + 1]

    over(0, total // WIN, group, short=total == WIN)

    over_peers(lambda j, c: peak_copy(j, c, me).start())
    final[me] = peaks[peak_row(chip, core)]
    over_peers(lambda j, c: peak_copy(chip, core, j * cores + c).wait_recv())

    high = lax.rem(lax.div(me, SUB), 2) * (WIN // 2)
    e_of = lax.broadcasted_iota(jnp.int32, (per_row, WIN), 0)
    l_of = lax.broadcasted_iota(jnp.int32, (per_row, WIN), 1)
    groups = count // per_row
    for g in range(groups):
        to = (g + groups // 2) % groups if groups > 1 else 0
        x = final[g * per_row:(g + 1) * per_row].reshape(per_row, WIN)
        x = pltpu.roll(x, lax.rem(WIN - high, WIN), 1)
        turn = 0 if groups > 1 else per_row // 2
        x = jnp.concatenate([
            pltpu.roll(x[h:h + SUB], (h + turn) * rows % WIN, 1, stride=rows, stride_axis=0)
            for h in range(0, per_row, SUB)], axis=0)
        for i in range(wins):
            y = pltpu.roll(x, (WIN - i * rows) % WIN, 1)
            y = jnp.where(lax.div(l_of, rows) == lax.rem(e_of + turn, per_row), y, 0.0)
            out_ref[i:i + 1, to * WIN:(to + 1) * WIN] = jnp.sum(y, axis=0, keepdims=True)

    bank_copy(across(chip), me, bank_s.at[0]).wait_send()
    over(1, near, lambda k: bank_copy(facing(k), me, bank_s.at[k]).wait_send())
    over(1, near, lambda k: bank_copy(facing(k), relay, fwd_s.at[k]).wait_send())

    def passed(j):
        for d in range(1, cores):
            pass_copy(j * cores + core, other_core(d)).wait_send()

    over(0, near, lambda k: passed(close(k)))
    over(0, near, lambda k: passed(across(close(k))))

    def drain(j, c):
        pow_copy(j, c, me).wait_send()
        peak_copy(j, c, me).wait_send()

    over_peers(drain)


def per_device(chips, cores, basis_series, reconstruction, offsets):
    dets, basis, block = basis_series.shape
    templates = reconstruction.shape[1]
    bank = reconstruction.reshape(dets, templates * 2, basis)
    count = chips * cores
    rows = templates // cores
    wins = block // WIN
    total = count * wins
    hbm = pl.BlockSpec(memory_space=pltpu.HBM)
    scratch = [
        pltpu.SMEM(offsets.shape, offsets.dtype),
        pltpu.VMEM(basis_series.shape, basis_series.dtype),
        pltpu.VMEM(bank.shape, bank.dtype),
        pltpu.VMEM((cores, dets * rows * 2 + 2 * SUB, basis), jnp.bfloat16),
        pltpu.VMEM((count, dets * rows * 2 + 2 * SUB, basis), jnp.bfloat16),
        pltpu.VMEM((count, dets, rows * 2, block // 2), CODE),
        pltpu.VMEM((count, dets, rows * 2, block // 2), CODE),
        pltpu.VMEM((dets, total + SLIDE_BLOCKS * wins, rows, WIN), jnp.float32),
        pltpu.VMEM((total // WIN * SUB, 1, WIN), jnp.float32),
        pltpu.VMEM((count, 1, WIN), jnp.float32),
    ]
    held = sum(math.prod(x.shape) * jnp.dtype(x.dtype).itemsize for x in scratch[1:-2])
    held += (count + total // WIN * SUB) * SUB * WIN * 4
    out = pl.pallas_call(
        functools.partial(kernel, chips, cores),
        out_shape=jax.ShapeDtypeStruct((wins, count * rows), jnp.float32),
        in_specs=[hbm, hbm, hbm],
        out_specs=pl.BlockSpec(memory_space=pltpu.VMEM),
        scratch_shapes=scratch + [
            pltpu.SemaphoreType.DMA((3,)),
            pltpu.SemaphoreType.DMA((chips,)),
            pltpu.SemaphoreType.DMA((chips,)),
        ] + [pltpu.SemaphoreType.DMA((count,)) for _ in range(6)],
        compiler_params=pltpu.CompilerParams(
            collective_id=0, has_side_effects=True, vmem_limit_bytes=held + (4 << 20)),
    )(*(pltpu.with_memory_space_constraint(x, pltpu.HBM) for x in (offsets, basis_series, bank)))
    return out.T


def solution(mesh):
    chips, cores = mesh.shape["tmpl"], mesh.shape["det"]
    in_specs = (
        P(None, None, ("groups", "tmpl", "det")),
        P(None, ("groups", "tmpl"), None, None),
        P("groups"),
    )
    out_specs = P(None, ("groups", "tmpl", "det"))
    return jax.shard_map(
        functools.partial(per_device, chips, cores),
        mesh=mesh, in_specs=in_specs, out_specs=out_specs, check_vma=False,
    )
```

time: 35.8 us -> 33 us (0.922)
  Pallas kernels: 34.3 us -> 32.2 us
  local copies, waits for them, and re-layouts: 1.28 us -> 0.6 us
    pallas_call x1, Pallas kernels: 34.3 us -> 32.2 us  [per_device(): pl.pallas_call(functools.partial(kernel, chips, cores), out_shape=jax.Sha...]
    unnamed x1, local copies, waits for them, and re-layouts: 1.28 us -> 0.6 us
where the time goes in v1:
time: 33 us; the launch traced here: 32.8 us
  Pallas kernels  32.2 us (98%)
  local copies, waits for them, and re-layouts  0.6 us (2%)
    pallas_call x1, Pallas kernels, per_device(): pl.pallas_call(functools.partial(kernel, chips, cores), out_shape=jax.Sha...  32.2 us

profile of v1, /device:TPU:0, one launch (start us, length us, event | category | flops | bytes accessed | tf_op | source)
XLA Modules:
  0.0 32.8 jit_solution(10920041798685102099)
XLA Ops:
  0.0 32.2 %shard_map.37 = f32[8,128]{1,0:T(8,128)S(1)} custom-call(s32[3]{0:T(128)} %off_hbm.1, bf16[3,128,1024]{2,1,0:T(8,128)(2,1)} %basis_hbm.1, bf16[3,32,128]{2,1,0:T(8,128)(2,1)} %bitcast.3), custom_call_target="tpu_custom_call" | custom-call | tf_op jit(solution)/shard_map/pallas_call | solution.py:371
  32.3 0.6 %copy.5 = f32[128,8]{0,1:T(8,128)} copy(f32[128,8]{0,1:T(8,128)S(1)} %bitcast.2) | data formatting | bytes 8192

commit v2 on v1

--- a/solution.py
+++ b/solution.py
@@ -11,6 +11,8 @@
 WIN = 128
 SUB = 8
 SLIDE_BLOCKS = 16
+SUMS = 16
+VMEM_MOST = 62 << 20
 MESH = pl.DeviceIdType.MESH
 TINY = 1e-18
 CODE = jnp.int16
@@ -31,10 +33,10 @@
 
 
 def kernel(
-    chips, cores,
+    chips, cores, adder,
     off_hbm, basis_hbm, bank_hbm, out_ref,
     off_ref, basis_ref, bank_ref, bank_own, bank_all, stage, recv, dec, peaks, final,
-    load, bank_s, fwd_s, pass_s, bank_r, pow_s, pow_r, peak_s, peak_r,
+    sums, added, part, load, bank_s, fwd_s, pass_s, bank_r, pow_s, pow_r, peak_s, peak_r, sum_s, sum_r,
 ):
     dets, basis, block = basis_ref.shape
     rows2 = bank_ref.shape[1] // cores
@@ -111,6 +113,30 @@
             send_sem=pow_s.at[j * cores + c], recv_sem=pow_r.at[src],
             device_id=dev(j, c), device_id_type=MESH)
 
+    def lift(i):
+        return lax.rem(i + near * cores, count)
+
+    def add_copy(j, src):
+        slot = across(j) * cores + adder
+        return pltpu.make_async_remote_copy(
+            src_ref=stage.at[slot], dst_ref=recv.at[lift(src)],
+            send_sem=pow_s.at[slot], recv_sem=pow_r.at[lift(src)],
+            device_id=dev(j, adder), device_id_type=MESH)
+
+    def sum_copy(q):
+        some = pl.ds(q * SUMS, SUMS)
+        return pltpu.make_async_remote_copy(
+            src_ref=sums.at[some], dst_ref=added.at[some], send_sem=sum_s.at[q], recv_sem=sum_r.at[q],
+            device_id=dev(across(chip), adder), device_id_type=MESH)
+
+    def cross(j, fn, own=False):
+        if adder is not None:
+            add = lambda: fn(add_copy(j, me))
+            pl.when(core != adder)(add) if own else add()
+        for c in range(cores):
+            if c != adder:
+                fn(pow_copy(across(j), c, me))
+
     def peak_row(j, c):
         i = j * cores + c
         return lax.div(i, per_row) * SUB + lax.rem(SUB - lax.rem(i, SUB), SUB)
@@ -142,15 +168,16 @@
     for c in range(cores):
         bank_own[c, :span] = sorted_bank[c * span:(c + 1) * span]
     load_basis.wait()
+    first_rows = lax.broadcasted_iota(jnp.int32, (SUB, basis), 0) < SUB // 2
     top = largest(basis_ref[...].reshape(dets * basis, block))
     for c in range(cores):
         own_max = largest(sorted_bank[c * span:(c + 1) * span])
-        note = jnp.concatenate([jnp.broadcast_to(top, (SUB, basis)), jnp.broadcast_to(own_max, (SUB, basis))], axis=0)
+        note = jnp.where(first_rows, jnp.broadcast_to(top, (SUB, basis)), jnp.broadcast_to(own_max, (SUB, basis)))
         bank_own[c, span:] = note.astype(jnp.bfloat16)
     bank_all[me] = bank_own[core]
 
     def bank_max(bank, src):
-        return bank[src, span + SUB:].astype(jnp.float32)[:1, :1]
+        return bank[src, span:].astype(jnp.float32)[SUB // 2:SUB // 2 + 1, :1]
 
     def powers_for(j, bank, first):
         to = across(j)
@@ -172,12 +199,20 @@
             fn(j * cores + other_core(d))
 
     powers_for(chip, bank_own, 0)
+    if adder is not None:
+        @pl.when(core == adder)
+        def _():
+            dec[...] = jnp.zeros_like(dec)
+
+        @pl.when(core != adder)
+        def _():
+            part[...] = jnp.zeros_like(part)
+
     pl.semaphore_wait(barrier, count - 1)
 
     bank_copy(across(chip), me, bank_s.at[0]).start()
     over(1, near, lambda k: bank_copy(facing(k), me, bank_s.at[k]).start())
-    for c in range(cores):
-        pow_copy(across(chip), c, me).start()
+    cross(chip, lambda copy: copy.start(), own=True)
     for d in range(1, cores):
         pass_copy(me, other_core(d)).start()
 
@@ -195,8 +230,7 @@
         j = close(k)
         pieces(j, lambda src: bank_copy(chip, src, bank_s.at[0]).wait_recv())
         powers_for(j, bank_all, j * cores)
-        for c in range(cores):
-            pow_copy(across(j), c, me).start()
+        cross(j, lambda copy: copy.start())
 
     over(1, near, near_powers, short=False)
 
@@ -218,11 +252,18 @@
     load_off.wait()
     rest = [lax.rem(off_ref[d], WIN) for d in range(dets)]
     shifts = [lax.div(off_ref[d], WIN) for d in range(dets)]
-    owned = bank_max(bank_all, across(chip) * cores + core)
-
-    def decode(src, value):
-        a = jnp.maximum(bank_all[src, span:span + SUB].astype(jnp.float32)[:1, :1] * owned, TINY)
-        scale = a * a
+    lane = lax.broadcasted_iota(jnp.int32, (rows, WIN), 1)
+    inside = [lane < WIN - rest[d] for d in range(dets)]
+
+    def top_of(src):
+        return bank_all[src, span:].astype(jnp.float32)[:1, :1]
+
+    def scale_of(top, bank):
+        a = jnp.maximum(top * bank, TINY)
+        return a * a
+
+    def decode(src, value, bank):
+        scale = scale_of(top_of(src), bank)
         for d in range(dets):
             x = decoded(value(d)) * scale
             tiles = []
@@ -238,39 +279,7 @@
                 for v in range(wins):
                     dec[d, (count + src) * wins + v] = tiles[v]
 
-    decode(me, lambda d: stage[me, d])
-
-    def take(j, c):
-        src = j * cores + c
-        pow_copy(chip, core, src).wait_recv()
-        decode(src, lambda d: recv[src, d])
-
-    @pl.loop(0, cores)
-    def _(c):
-        take(across(chip), c)
-
-    pieces(chip, lambda src: bank_copy(chip, src, bank_s.at[0]).wait_recv())
-    for d in range(1, cores):
-        take(chip, other_core(d))
-
-    def take_pair(k):
-        @pl.loop(0, 2 * cores)
-        def _(n):
-            far = lax.div(n, cores)
-            j = lax.rem(facing(k) + far * near, chips)
-            take(j, lax.rem(n, cores))
-
-    over(1, near, take_pair, short=False)
-
-    lane = lax.broadcasted_iota(jnp.int32, (rows, WIN), 1)
-    inside = [lane < WIN - rest[d] for d in range(dets)]
-    bit = [lax.rem(lax.div(lane, 1 << p), 2) == 0 for p in range(7)]
-    row = lax.broadcasted_iota(jnp.int32, (rows, WIN), 0)
-    dest = lax.rem(SUB - row, SUB) + SUB * lax.div(lane, WIN // 2)
-    index = SUB * lax.rem(dest + lax.rem(lane, SUB), per_row) + lax.rem(lax.div(lane, SUB), SUB)
-
-    def group(g):
-        base = g * WIN
+    def adding(base):
         last = {}
 
         def tile(d, v):
@@ -285,6 +294,92 @@
                 x = jnp.where(inside[d], lo, tile(d, v + 1))
                 power = x if power is None else power + x
             return power
+
+        return leaf
+
+    def far_take():
+        @pl.loop(0, near * cores)
+        def _(n):
+            src = across(close(lax.div(n, cores))) * cores + lax.rem(n, cores)
+            pow_copy(chip, core, src).wait_recv()
+            decode(src, lambda d: recv[src, d], owned)
+
+    def add_near():
+        bank = bank_max(bank_all, me)
+        decode(me, lambda d: stage[lift(me), d], bank)
+
+        def take(src):
+            pow_copy(chip, core, lift(src)).wait_recv()
+            decode(src, lambda d: recv[lift(src), d], bank)
+
+        for d in range(1, cores):
+            take(chip * cores + other_core(d))
+
+        @pl.loop(cores, near * cores)
+        def _(n):
+            take(close(lax.div(n, cores)) * cores + lax.rem(n, cores))
+
+        inv = 1.0 / (4.0 * scale_of(most(lambda k: close(k)), bank))
+
+        @pl.loop(0, total // 2 // SUMS)
+        def _(q):
+            leaf = adding(q * 2 * SUMS)
+            for v in range(SUMS):
+                pair = jnp.concatenate([leaf(2 * v), leaf(2 * v + 1)], axis=0)
+                sums[q * SUMS + v] = coded(pair * inv)
+            sum_copy(q).start()
+
+    def most(chip_of):
+        tops = [bank_all[chip_of(k) * cores + c, span:] for k in range(near) for c in range(cores)]
+        return functools.reduce(jnp.maximum, [x.astype(jnp.float32) for x in tops])[:1, :1]
+
+    def take_sums():
+        scale = 4.0 * scale_of(most(lambda k: across(close(k))), owned)
+
+        @pl.loop(0, total // 2 // SUMS)
+        def _(q):
+            sum_copy(q).wait_recv()
+            for v in range(SUMS):
+                x = decoded(added[q * SUMS + v]) * scale
+                part[(q * SUMS + v) * 2] = x[:rows]
+                part[(q * SUMS + v) * 2 + 1] = x[rows:]
+
+    pieces(chip, lambda src: bank_copy(chip, src, bank_s.at[0]).wait_recv())
+    owned = bank_max(bank_all, across(chip) * cores + core)
+    if adder is None:
+        far_take()
+    else:
+        pl.when(core == adder)(add_near)
+        pl.when(core != adder)(far_take)
+
+    decode(me, lambda d: stage[me, d], owned)
+
+    def take(j, c):
+        src = j * cores + c
+        pow_copy(chip, core, src).wait_recv()
+        decode(src, lambda d: recv[src, d], owned)
+
+    for d in range(1, cores):
+        take(chip, other_core(d))
+
+    @pl.loop(cores, near * cores)
+    def _(n):
+        take(close(lax.div(n, cores)), lax.rem(n, cores))
+
+    if adder is not None:
+        pl.when(core == adder)(take_sums)
+
+    bit = [lax.rem(lax.div(lane, 1 << p), 2) == 0 for p in range(7)]
+    row = lax.broadcasted_iota(jnp.int32, (rows, WIN), 0)
+    dest = lax.rem(SUB - row, SUB) + SUB * lax.div(lane, WIN // 2)
+    index = SUB * lax.rem(dest + lax.rem(lane, SUB), per_row) + lax.rem(lax.div(lane, SUB), SUB)
+
+    def group(g):
+        base = g * WIN
+        near_sum = adding(base)
+
+        def leaf(v):
+            return near_sum(v) if adder is None else near_sum(v) + part[base + v]
 
         def merged(k, v):
             if k == 0:
@@ -338,11 +433,22 @@
     over(0, near, lambda k: passed(close(k)))
     over(0, near, lambda k: passed(across(close(k))))
 
-    def drain(j, c):
-        pow_copy(j, c, me).wait_send()
-        peak_copy(j, c, me).wait_send()
-
-    over_peers(drain)
+    def drain(k):
+        j = close(k)
+        for c in range(cores):
+            pow_copy(j, c, me).wait_send()
+
+    over(1, near, drain)
+    for d in range(1, cores):
+        pow_copy(chip, other_core(d), me).wait_send()
+    cross(chip, lambda copy: copy.wait_send(), own=True)
+    over(1, near, lambda k: cross(close(k), lambda copy: copy.wait_send()))
+    over_peers(lambda j, c: peak_copy(j, c, me).wait_send())
+    if adder is not None:
+        @pl.when(core == adder)
+        def _():
+            for q in range(total // 2 // SUMS):
+                sum_copy(q).wait_send()
 
 
 def per_device(chips, cores, basis_series, reconstruction, offsets):
@@ -358,8 +464,8 @@
         pltpu.SMEM(offsets.shape, offsets.dtype),
         pltpu.VMEM(basis_series.shape, basis_series.dtype),
         pltpu.VMEM(bank.shape, bank.dtype),
-        pltpu.VMEM((cores, dets * rows * 2 + 2 * SUB, basis), jnp.bfloat16),
-        pltpu.VMEM((count, dets * rows * 2 + 2 * SUB, basis), jnp.bfloat16),
+        pltpu.VMEM((cores, dets * rows * 2 + SUB, basis), jnp.bfloat16),
+        pltpu.VMEM((count, dets * rows * 2 + SUB, basis), jnp.bfloat16),
         pltpu.VMEM((count, dets, rows * 2, block // 2), CODE),
         pltpu.VMEM((count, dets, rows * 2, block // 2), CODE),
         pltpu.VMEM((dets, total + SLIDE_BLOCKS * wins, rows, WIN), jnp.float32),
@@ -367,9 +473,18 @@
         pltpu.VMEM((count, 1, WIN), jnp.float32),
     ]
     held = sum(math.prod(x.shape) * jnp.dtype(x.dtype).itemsize for x in scratch[1:-2])
-    held += (count + total // WIN * SUB) * SUB * WIN * 4
+    held += (count + total // WIN * SUB) * SUB * WIN * 4 + (4 << 20)
+    extra = total * rows * WIN * 8
+    adder = cores - 1 if held + extra <= VMEM_MOST and cores > 1 else None
+    tiles = total if adder is not None else 2 * SUMS
+    scratch += [
+        pltpu.VMEM((tiles // 2, rows * 2, WIN), CODE),
+        pltpu.VMEM((tiles // 2, rows * 2, WIN), CODE),
+        pltpu.VMEM((tiles, rows, WIN), jnp.float32),
+    ]
+    held += tiles * rows * WIN * 8
     out = pl.pallas_call(
-        functools.partial(kernel, chips, cores),
+        functools.partial(kernel, chips, cores, adder),
         out_shape=jax.ShapeDtypeStruct((wins, count * rows), jnp.float32),
         in_specs=[hbm, hbm, hbm],
         out_specs=pl.BlockSpec(memory_space=pltpu.VMEM),
@@ -377,9 +492,10 @@
             pltpu.SemaphoreType.DMA((3,)),
             pltpu.SemaphoreType.DMA((chips,)),
             pltpu.SemaphoreType.DMA((chips,)),
-        ] + [pltpu.SemaphoreType.DMA((count,)) for _ in range(6)],
+        ] + [pltpu.SemaphoreType.DMA((count,)) for _ in range(6)]
+        + [pltpu.SemaphoreType.DMA((tiles // 2 // SUMS,)) for _ in range(2)],
         compiler_params=pltpu.CompilerParams(
-            collective_id=0, has_side_effects=True, vmem_limit_bytes=held + (4 << 20)),
+            collective_id=0, has_side_effects=True, vmem_limit_bytes=held),
     )(*(pltpu.with_memory_space_constraint(x, pltpu.HBM) for x in (offsets, basis_series, bank)))
     return out.T
 

time: 33 us -> 32 us (0.970)
  Pallas kernels: 32.2 us -> 31.2 us
    pallas_call x1, Pallas kernels: 32.2 us -> 31.2 us  [per_device(): pl.pallas_call(functools.partial(kernel, chips, cores, adder), out_shape=...]
where the time goes in v2:
time: 32 us; the launch traced here: 31.9 us
  Pallas kernels  31.2 us (98%)
  local copies, waits for them, and re-layouts  0.6 us (2%)
    pallas_call x1, Pallas kernels, per_device(): pl.pallas_call(functools.partial(kernel, chips, cores, adder), out_shape=...  31.2 us

profile of v2, /device:TPU:0, one launch (start us, length us, event | category | flops | bytes accessed | tf_op | source)
XLA Modules:
  0.0 31.9 jit_solution(12896622027852840556)
XLA Ops:
  0.0 31.2 %shard_map.37 = f32[8,128]{1,0:T(8,128)S(1)} custom-call(s32[3]{0:T(128)} %off_hbm.1, bf16[3,128,1024]{2,1,0:T(8,128)(2,1)} %basis_hbm.1, bf16[3,32,128]{2,1,0:T(8,128)(2,1)} %bitcast.3), custom_call_target="tpu_custom_call" | custom-call | tf_op jit(solution)/shard_map/pallas_call | solution.py:486
  31.3 0.6 %copy.5 = f32[128,8]{0,1:T(8,128)} copy(f32[128,8]{0,1:T(8,128)S(1)} %bitcast.2) | data formatting | bytes 8192

commit v3 on v2

--- a/solution.py
+++ b/solution.py
@@ -36,7 +36,7 @@
     chips, cores, adder,
     off_hbm, basis_hbm, bank_hbm, out_ref,
     off_ref, basis_ref, bank_ref, bank_own, bank_all, stage, recv, dec, peaks, final,
-    sums, added, part, load, bank_s, fwd_s, pass_s, bank_r, pow_s, pow_r, peak_s, peak_r, sum_s, sum_r,
+    sums, added, part, load, sent, bank_r, pow_r, peak_r, sum_r,
 ):
     dets, basis, block = basis_ref.shape
     rows2 = bank_ref.shape[1] // cores
@@ -65,12 +65,7 @@
         return lax.rem(j + near, chips)
 
     def close(k):
-        if near & (near - 1):
-            return side * near + lax.rem(place + near + k, near)
         return side * near + lax.bitwise_xor(place, jnp.int32(k))
-
-    def facing(k):
-        return close(-k if near & (near - 1) else k)
 
     def other_core(d):
         return lax.rem(core + d, cores)
@@ -96,22 +91,27 @@
     barrier = pltpu.get_barrier_semaphore()
     over_peers(lambda j, c: pl.semaphore_signal(barrier, inc=1, device_id=dev(j, c), device_id_type=MESH))
 
-    def bank_copy(j, src, sem):
-        return pltpu.make_async_remote_copy(
-            src_ref=bank_all.at[src], dst_ref=bank_all.at[src], send_sem=sem, recv_sem=bank_r.at[src],
+    def bank_copy(j, src):
+        return pltpu.make_async_remote_copy(
+            src_ref=bank_all.at[src], dst_ref=bank_all.at[src], send_sem=sent.at[0], recv_sem=bank_r.at[src],
             device_id=dev(j, core), device_id_type=MESH)
 
     def pass_copy(src, c):
         return pltpu.make_async_remote_copy(
             src_ref=bank_all.at[src], dst_ref=bank_all.at[src],
-            send_sem=pass_s.at[lax.div(src, cores) * cores + c], recv_sem=bank_r.at[src],
+            send_sem=sent.at[0], recv_sem=bank_r.at[src],
             device_id=dev(chip, c), device_id_type=MESH)
 
     def pow_copy(j, c, src):
         return pltpu.make_async_remote_copy(
             src_ref=stage.at[j * cores + c], dst_ref=recv.at[src],
-            send_sem=pow_s.at[j * cores + c], recv_sem=pow_r.at[src],
+            send_sem=sent.at[1], recv_sem=pow_r.at[src],
             device_id=dev(j, c), device_id_type=MESH)
+
+    def over_all(ref, sem, n):
+        some = ref.at[pl.ds(0, n)]
+        return pltpu.make_async_remote_copy(
+            src_ref=some, dst_ref=some, send_sem=sem, recv_sem=sem, device_id=dev(chip, core), device_id_type=MESH)
 
     def lift(i):
         return lax.rem(i + near * cores, count)
@@ -120,14 +120,23 @@
         slot = across(j) * cores + adder
         return pltpu.make_async_remote_copy(
             src_ref=stage.at[slot], dst_ref=recv.at[lift(src)],
-            send_sem=pow_s.at[slot], recv_sem=pow_r.at[lift(src)],
+            send_sem=sent.at[1], recv_sem=pow_r.at[lift(src)],
             device_id=dev(j, adder), device_id_type=MESH)
 
     def sum_copy(q):
         some = pl.ds(q * SUMS, SUMS)
         return pltpu.make_async_remote_copy(
-            src_ref=sums.at[some], dst_ref=added.at[some], send_sem=sum_s.at[q], recv_sem=sum_r.at[q],
+            src_ref=sums.at[some], dst_ref=added.at[some], send_sem=sent.at[3], recv_sem=sum_r.at[q],
             device_id=dev(across(chip), adder), device_id_type=MESH)
+
+    def near_copy(j, c):
+        e = 0 if adder is None else lax.div(c, jnp.int32(adder))
+        slot = across(j) * cores + c
+        src = lax.rem(me + e * near * cores, count)
+        return pltpu.make_async_remote_copy(
+            src_ref=stage.at[slot], dst_ref=recv.at[src],
+            send_sem=sent.at[1], recv_sem=pow_r.at[src],
+            device_id=dev(lax.rem(j + (1 - e) * near, chips), c), device_id_type=MESH)
 
     def cross(j, fn, own=False):
         if adder is not None:
@@ -144,7 +153,7 @@
     def peak_copy(j, c, src):
         return pltpu.make_async_remote_copy(
             src_ref=peaks.at[peak_row(j, c)], dst_ref=final.at[src],
-            send_sem=peak_s.at[j * cores + c], recv_sem=peak_r.at[src],
+            send_sem=sent.at[2], recv_sem=peak_r.at[0],
             device_id=dev(j, c), device_id_type=MESH)
 
     span = dets * rows2
@@ -199,6 +208,14 @@
             fn(j * cores + other_core(d))
 
     powers_for(chip, bank_own, 0)
+    pl.semaphore_wait(barrier, count - 1)
+
+    bank_copy(across(chip), me).start()
+    over(1, near, lambda k: bank_copy(close(k), me).start())
+    cross(chip, lambda copy: copy.start(), own=True)
+    for d in range(1, cores):
+        pass_copy(me, other_core(d)).start()
+
     if adder is not None:
         @pl.when(core == adder)
         def _():
@@ -208,47 +225,40 @@
         def _():
             part[...] = jnp.zeros_like(part)
 
-    pl.semaphore_wait(barrier, count - 1)
-
-    bank_copy(across(chip), me, bank_s.at[0]).start()
-    over(1, near, lambda k: bank_copy(facing(k), me, bank_s.at[k]).start())
-    cross(chip, lambda copy: copy.start(), own=True)
-    for d in range(1, cores):
-        pass_copy(me, other_core(d)).start()
 
     def pass_on(src):
-        bank_copy(chip, src, bank_s.at[0]).wait_recv()
+        bank_copy(chip, src).wait_recv()
         for d in range(1, cores):
             pass_copy(src, other_core(d)).start()
 
-    over(1, near, lambda k: pass_on(close(k) * cores + core))
+    def piece_powers(j, c):
+        a = jnp.maximum(bank_max(bank_all, j * cores + c) * top, TINY)
+        inv = 1.0 / (a * a)
+        for d in range(dets):
+            f = jnp.dot(
+                bank_all[j * cores + c, d * rows2:(d + 1) * rows2], basis_ref[d], preferred_element_type=jnp.float32)
+            f = f * f
+            p = (f[:rows] + f[rows:]) * inv
+            stage[across(j) * cores + c, d] = coded(jnp.concatenate([p[:, :half], p[:, half:]], axis=0))
+        near_copy(j, c).start()
+
+    def near_direct(k):
+        pass_on(close(k) * cores + core)
+        piece_powers(close(k), core)
+
+    def near_passed(k):
+        for d in range(1, cores):
+            bank_copy(chip, close(k) * cores + other_core(d)).wait_recv()
+            piece_powers(close(k), other_core(d))
+
+    over(1, near // 2, near_direct)
     relay = across(chip) * cores + core
     pass_on(relay)
-    over(1, near, lambda k: bank_copy(facing(k), relay, fwd_s.at[k]).start())
-
-    def near_powers(k):
-        j = close(k)
-        pieces(j, lambda src: bank_copy(chip, src, bank_s.at[0]).wait_recv())
-        powers_for(j, bank_all, j * cores)
-        cross(j, lambda copy: copy.start())
-
-    over(1, near, near_powers, short=False)
+    over(1, near, lambda k: bank_copy(close(k), relay).start())
+    over(near // 2, near, near_direct)
+    over(1, near, near_passed, short=False)
 
     over(1, near, lambda k: pass_on(across(close(k)) * cores + core))
-    pieces(across(chip), lambda src: bank_copy(chip, src, bank_s.at[0]).wait_recv())
-    powers_for(across(chip), bank_all, across(chip) * cores)
-    for d in range(1, cores):
-        pow_copy(chip, other_core(d), me).start()
-
-    def far_powers(k):
-        j = across(close(k))
-        pieces(j, lambda src: bank_copy(chip, src, bank_s.at[0]).wait_recv())
-        powers_for(j, bank_all, j * cores)
-        for c in range(cores):
-            pow_copy(close(k), c, me).start()
-
-    over(1, near, far_powers, short=False)
-
     load_off.wait()
     rest = [lax.rem(off_ref[d], WIN) for d in range(dets)]
     shifts = [lax.div(off_ref[d], WIN) for d in range(dets)]
@@ -344,12 +354,28 @@
                 part[(q * SUMS + v) * 2] = x[:rows]
                 part[(q * SUMS + v) * 2 + 1] = x[rows:]
 
-    pieces(chip, lambda src: bank_copy(chip, src, bank_s.at[0]).wait_recv())
+    pieces(chip, lambda src: bank_copy(chip, src).wait_recv())
     owned = bank_max(bank_all, across(chip) * cores + core)
+    if adder is not None:
+        pl.when(core == adder)(add_near)
+
+    pieces(across(chip), lambda src: bank_copy(chip, src).wait_recv())
+    powers_for(across(chip), bank_all, across(chip) * cores)
+    for d in range(1, cores):
+        pow_copy(chip, other_core(d), me).start()
+
+    def far_powers(k):
+        j = across(close(k))
+        pieces(j, lambda src: bank_copy(chip, src).wait_recv())
+        powers_for(j, bank_all, j * cores)
+        for c in range(cores):
+            pow_copy(close(k), c, me).start()
+
+    over(1, near, far_powers, short=False)
+
     if adder is None:
         far_take()
     else:
-        pl.when(core == adder)(add_near)
         pl.when(core != adder)(far_take)
 
     decode(me, lambda d: stage[me, d], owned)
@@ -403,7 +429,7 @@
 
     over_peers(lambda j, c: peak_copy(j, c, me).start())
     final[me] = peaks[peak_row(chip, core)]
-    over_peers(lambda j, c: peak_copy(chip, core, j * cores + c).wait_recv())
+    over_all(final, peak_r.at[0], count - 1).wait_recv()
 
     high = lax.rem(lax.div(me, SUB), 2) * (WIN // 2)
     e_of = lax.broadcasted_iota(jnp.int32, (per_row, WIN), 0)
@@ -422,33 +448,20 @@
             y = jnp.where(lax.div(l_of, rows) == lax.rem(e_of + turn, per_row), y, 0.0)
             out_ref[i:i + 1, to * WIN:(to + 1) * WIN] = jnp.sum(y, axis=0, keepdims=True)
 
-    bank_copy(across(chip), me, bank_s.at[0]).wait_send()
-    over(1, near, lambda k: bank_copy(facing(k), me, bank_s.at[k]).wait_send())
-    over(1, near, lambda k: bank_copy(facing(k), relay, fwd_s.at[k]).wait_send())
-
-    def passed(j):
-        for d in range(1, cores):
-            pass_copy(j * cores + core, other_core(d)).wait_send()
-
-    over(0, near, lambda k: passed(close(k)))
-    over(0, near, lambda k: passed(across(close(k))))
-
-    def drain(k):
-        j = close(k)
-        for c in range(cores):
-            pow_copy(j, c, me).wait_send()
-
-    over(1, near, drain)
-    for d in range(1, cores):
-        pow_copy(chip, other_core(d), me).wait_send()
-    cross(chip, lambda copy: copy.wait_send(), own=True)
-    over(1, near, lambda k: cross(close(k), lambda copy: copy.wait_send()))
-    over_peers(lambda j, c: peak_copy(j, c, me).wait_send())
-    if adder is not None:
+    banks = near + (near - 1) + chips * (cores - 1)
+    over_all(bank_all, sent.at[0], banks).wait_send()
+    over_all(final, sent.at[2], count - 1).wait_send()
+    if adder is None:
+        over_all(stage, sent.at[1], count - 1).wait_send()
+    else:
         @pl.when(core == adder)
         def _():
-            for q in range(total // 2 // SUMS):
-                sum_copy(q).wait_send()
+            over_all(stage, sent.at[1], count - 2).wait_send()
+            over_all(sums, sent.at[3], total // 2).wait_send()
+
+        @pl.when(core != adder)
+        def _():
+            over_all(stage, sent.at[1], count - 1).wait_send()
 
 
 def per_device(chips, cores, basis_series, reconstruction, offsets):
@@ -490,10 +503,12 @@
         out_specs=pl.BlockSpec(memory_space=pltpu.VMEM),
         scratch_shapes=scratch + [
             pltpu.SemaphoreType.DMA((3,)),
-            pltpu.SemaphoreType.DMA((chips,)),
-            pltpu.SemaphoreType.DMA((chips,)),
-        ] + [pltpu.SemaphoreType.DMA((count,)) for _ in range(6)]
-        + [pltpu.SemaphoreType.DMA((tiles // 2 // SUMS,)) for _ in range(2)],
+            pltpu.SemaphoreType.DMA((4,)),
+            pltpu.SemaphoreType.DMA((count,)),
+            pltpu.SemaphoreType.DMA((count,)),
+            pltpu.SemaphoreType.DMA((1,)),
+            pltpu.SemaphoreType.DMA((tiles // 2 // SUMS,)),
+        ],
         compiler_params=pltpu.CompilerParams(
             collective_id=0, has_side_effects=True, vmem_limit_bytes=held),
     )(*(pltpu.with_memory_space_constraint(x, pltpu.HBM) for x in (offsets, basis_series, bank)))

time: 32 us -> 30.6 us (0.956)
  Pallas kernels: 31.2 us -> 29.8 us
    pallas_call x1, Pallas kernels: 31.2 us -> 29.8 us  [per_device(): pl.pallas_call(functools.partial(kernel, chips, cores, adder), out_shape=...]
where the time goes in v3:
time: 30.6 us; the launch traced here: 30.4 us
  Pallas kernels  29.8 us (97%)
  local copies, waits for them, and re-layouts  0.6 us (2%)
    pallas_call x1, Pallas kernels, per_device(): pl.pallas_call(functools.partial(kernel, chips, cores, adder), out_shape=...  29.8 us

profile of v3, /device:TPU:0, one launch (start us, length us, event | category | flops | bytes accessed | tf_op | source)
XLA Modules:
  0.0 30.4 jit_solution(6017917119990044396)
XLA Ops:
  0.0 29.8 %shard_map.37 = f32[8,128]{1,0:T(8,128)S(1)} custom-call(s32[3]{0:T(128)} %off_hbm.1, bf16[3,128,1024]{2,1,0:T(8,128)(2,1)} %basis_hbm.1, bf16[3,32,128]{2,1,0:T(8,128)(2,1)} %bitcast.3), custom_call_target="tpu_custom_call" | custom-call | tf_op jit(solution)/shard_map/pallas_call | solution.py:499
  29.8 0.6 %copy.5 = f32[128,8]{0,1:T(8,128)} copy(f32[128,8]{0,1:T(8,128)S(1)} %bitcast.2) | data formatting | bytes 8192

commit v4 on v3

--- a/solution.py
+++ b/solution.py
@@ -240,23 +240,36 @@
             f = f * f
             p = (f[:rows] + f[rows:]) * inv
             stage[across(j) * cores + c, d] = coded(jnp.concatenate([p[:, :half], p[:, half:]], axis=0))
-        near_copy(j, c).start()
-
-    def near_direct(k):
+
+    def near_direct(k, hold=False):
         pass_on(close(k) * cores + core)
         piece_powers(close(k), core)
+        copy = near_copy(close(k), core)
+        if not hold or adder is None:
+            copy.start()
+        else:
+            pl.when(core == adder)(copy.start)
 
     def near_passed(k):
         for d in range(1, cores):
             bank_copy(chip, close(k) * cores + other_core(d)).wait_recv()
             piece_powers(close(k), other_core(d))
-
-    over(1, near // 2, near_direct)
+            near_copy(close(k), other_core(d)).start()
+
+    near_direct(near // 2)
     relay = across(chip) * cores + core
     pass_on(relay)
     over(1, near, lambda k: bank_copy(close(k), relay).start())
-    over(near // 2, near, near_direct)
+    over(1, near // 2, lambda k: near_direct(near - k, True))
+    over(1, near // 2, lambda k: near_direct(near // 2 - k, True))
     over(1, near, near_passed, short=False)
+
+    def release(k):
+        if adder is not None:
+            pl.when(core != adder)(near_copy(close(k), core).start)
+
+    over(1, near // 2, lambda k: release(near - k))
+    over(1, near // 2, lambda k: release(near // 2 - k))
 
     over(1, near, lambda k: pass_on(across(close(k)) * cores + core))
     load_off.wait()

time: 30.6 us -> 29.7 us (0.971)
  Pallas kernels: 29.8 us -> 28.9 us
    pallas_call x1, Pallas kernels: 29.8 us -> 28.9 us  [per_device(): pl.pallas_call(functools.partial(kernel, chips, cores, adder), out_shape=...]
where the time goes in v4:
time: 29.7 us; the launch traced here: 29.5 us
  Pallas kernels  28.9 us (97%)
  local copies, waits for them, and re-layouts  0.6 us (2%)
    pallas_call x1, Pallas kernels, per_device(): pl.pallas_call(functools.partial(kernel, chips, cores, adder), out_shape=...  28.9 us
    unnamed x1, local copies, waits for them, and re-layouts  0.6 us

profile of v4, /device:TPU:0, one launch (start us, length us, event | category | flops | bytes accessed | tf_op | source)
XLA Modules:
  0.0 29.5 jit_solution(2042251506157431195)
XLA Ops:
  0.0 28.9 %shard_map.37 = f32[8,128]{1,0:T(8,128)S(1)} custom-call(s32[3]{0:T(128)} %off_hbm.1, bf16[3,128,1024]{2,1,0:T(8,128)(2,1)} %basis_hbm.1, bf16[3,32,128]{2,1,0:T(8,128)(2,1)} %bitcast.3), custom_call_target="tpu_custom_call" | custom-call | tf_op jit(solution)/shard_map/pallas_call | solution.py:512
  28.9 0.6 %copy.5 = f32[128,8]{0,1:T(8,128)} copy(f32[128,8]{0,1:T(8,128)S(1)} %bitcast.2) | data formatting | bytes 8192

commit v5 on v4

--- a/solution.py
+++ b/solution.py
@@ -216,6 +216,13 @@
     for d in range(1, cores):
         pass_copy(me, other_core(d)).start()
 
+    def clear_edges():
+        @pl.loop(0, count + SLIDE_BLOCKS)
+        def _(n):
+            for d in range(dets):
+                dec[d, n * wins + wins - 1] = jnp.zeros((rows, WIN), jnp.float32)
+
+    clear_edges()
     if adder is not None:
         @pl.when(core == adder)
         def _():
@@ -285,36 +292,41 @@
         a = jnp.maximum(top * bank, TINY)
         return a * a
 
+    def kept(index, fn):
+        fn(index)
+        copied = lambda: fn(total + index)
+        copied() if count <= SLIDE_BLOCKS else pl.when(index < SLIDE_BLOCKS * wins)(copied)
+
     def decode(src, value, bank):
         scale = scale_of(top_of(src), bank)
+        first = src * wins
+        before = lax.rem(first + total - 1, total)
         for d in range(dets):
             x = decoded(value(d)) * scale
             tiles = []
             for v in range(wins):
                 h, q = divmod(v, wins // 2)
                 tile = x[h * rows:(h + 1) * rows, q * WIN:(q + 1) * WIN]
-                tile = pltpu.roll(tile, WIN - rest[d], 1)
-                dec[d, src * wins + v] = tile
-                tiles.append(tile)
-
-            @pl.when(src < SLIDE_BLOCKS)
-            def _():
-                for v in range(wins):
-                    dec[d, (count + src) * wins + v] = tiles[v]
+                tiles.append(pltpu.roll(tile, WIN - rest[d], 1))
+            head = jnp.where(inside[d], 0.0, tiles[0])
+            tail = jnp.where(inside[d], tiles[-1], 0.0)
+
+            def joined(at):
+                for v in range(wins - 1):
+                    dec[d, at + v] = jnp.where(inside[d], tiles[v], tiles[v + 1])
+                dec[d, at + wins - 1] += tail
+
+            def ahead(at):
+                dec[d, at] += head
+
+            kept(first, joined)
+            kept(before, ahead)
 
     def adding(base):
-        last = {}
-
-        def tile(d, v):
-            if last.get(d, (None, None))[0] != v:
-                last[d] = (v, dec[d, base + shifts[d] + v])
-            return last[d][1]
-
         def leaf(v):
             power = None
             for d in range(dets):
-                lo = tile(d, v)
-                x = jnp.where(inside[d], lo, tile(d, v + 1))
+                x = dec[d, base + shifts[d] + v]
                 power = x if power is None else power + x
             return power
 
@@ -352,6 +364,8 @@
                 sums[q * SUMS + v] = coded(pair * inv)
             sum_copy(q).start()
 
+        clear_edges()
+
     def most(chip_of):
         tops = [bank_all[chip_of(k) * cores + c, span:] for k in range(near) for c in range(cores)]
         return functools.reduce(jnp.maximum, [x.astype(jnp.float32) for x in tops])[:1, :1]
@@ -408,7 +422,6 @@
     if adder is not None:
         pl.when(core == adder)(take_sums)
 
-    bit = [lax.rem(lax.div(lane, 1 << p), 2) == 0 for p in range(7)]
     row = lax.broadcasted_iota(jnp.int32, (rows, WIN), 0)
     dest = lax.rem(SUB - row, SUB) + SUB * lax.div(lane, WIN // 2)
     index = SUB * lax.rem(dest + lax.rem(lane, SUB), per_row) + lax.rem(lax.div(lane, SUB), SUB)
@@ -420,20 +433,14 @@
         def leaf(v):
             return near_sum(v) if adder is None else near_sum(v) + part[base + v]
 
-        def merged(k, v):
-            if k == 0:
-                return leaf(v)
-            p = k - 1
-            a = merged(p, v)
-            b = merged(p, v + (1 << p))
-            s = jnp.where(bit[p], a, b)
-            t = jnp.where(bit[p], b, a)
-            return jnp.maximum(s, pltpu.roll(t, WIN - (1 << p), 1))
-
-        x = jnp.sqrt(merged(7, 0))
+        x = jnp.zeros((rows, WIN), jnp.float32)
+        for v in range(WIN):
+            x = jnp.where(lane == v, jnp.max(leaf(v), axis=1, keepdims=True), x)
+        x = jnp.sqrt(x)
         x = pltpu.roll(x, 0, 1, stride=SUB, stride_axis=0)
         for p in range(3):
-            x = jnp.where(bit[3 + p], x, pltpu.roll(x, SUB - (1 << p), 0))
+            stay = lax.rem(lax.div(lane, SUB << p), 2) == 0
+            x = jnp.where(stay, x, pltpu.roll(x, SUB - (1 << p), 0))
         x = jnp.take_along_axis(x, index, axis=1)
         for s in range(SUB):
             peaks[g * SUB + s] = x[s:s + 1]

time: 29.7 us -> 29.3 us (0.987)
  Pallas kernels: 28.9 us -> 28.5 us
    pallas_call x1, Pallas kernels: 28.9 us -> 28.5 us  [per_device(): pl.pallas_call(functools.partial(kernel, chips, cores, adder), out_shape=...]
where the time goes in v5:
time: 29.3 us; the launch traced here: 29.1 us
  Pallas kernels  28.5 us (97%)
  local copies, waits for them, and re-layouts  0.6 us (2%)
    pallas_call x1, Pallas kernels, per_device(): pl.pallas_call(functools.partial(kernel, chips, cores, adder), out_shape=...  28.5 us
    unnamed x1, local copies, waits for them, and re-layouts  0.6 us

profile of v5, /device:TPU:0, one launch (start us, length us, event | category | flops | bytes accessed | tf_op | source)
XLA Modules:
  0.0 29.1 jit_solution(14388013322355238011)
XLA Ops:
  0.0 28.5 %shard_map.37 = f32[8,128]{1,0:T(8,128)S(1)} custom-call(s32[3]{0:T(128)} %off_hbm.1, bf16[3,128,1024]{2,1,0:T(8,128)(2,1)} %basis_hbm.1, bf16[3,32,128]{2,1,0:T(8,128)(2,1)} %bitcast.3), custom_call_target="tpu_custom_call" | custom-call | tf_op jit(solution)/shard_map/pallas_call | solution.py:519
  28.5 0.6 %copy.5 = f32[128,8]{0,1:T(8,128)} copy(f32[128,8]{0,1:T(8,128)S(1)} %bitcast.2) | data formatting | bytes 8192

commit v6 on v5

--- a/solution.py
+++ b/solution.py
@@ -11,7 +11,7 @@
 WIN = 128
 SUB = 8
 SLIDE_BLOCKS = 16
-SUMS = 16
+SUMS = 32
 VMEM_MOST = 62 << 20
 MESH = pl.DeviceIdType.MESH
 TINY = 1e-18
@@ -81,12 +81,12 @@
             fn(k)
 
     def over_peers(fn):
+        for d in range(cores):
+            over(0, near, lambda k: fn(across(close(k)), other_core(d)))
+        for d in range(cores):
+            over(1, near, lambda k: fn(close(k), other_core(d)))
         for d in range(1, cores):
             fn(chip, other_core(d))
-        for d in range(cores):
-            c = other_core(d)
-            over(0, near, lambda k: fn(across(close(k)), c))
-            over(1, near, lambda k: fn(close(k), c))
 
     barrier = pltpu.get_barrier_semaphore()
     over_peers(lambda j, c: pl.semaphore_signal(barrier, inc=1, device_id=dev(j, c), device_id_type=MESH))
@@ -398,7 +398,7 @@
         for c in range(cores):
             pow_copy(close(k), c, me).start()
 
-    over(1, near, far_powers, short=False)
+    over(1, near, lambda k: far_powers(near - k), short=False)
 
     if adder is None:
         far_take()
@@ -449,6 +449,20 @@
 
     over_peers(lambda j, c: peak_copy(j, c, me).start())
     final[me] = peaks[peak_row(chip, core)]
+    banks = near + (near - 1) + chips * (cores - 1)
+    over_all(bank_all, sent.at[0], banks).wait_send()
+    if adder is None:
+        over_all(stage, sent.at[1], count - 1).wait_send()
+    else:
+        @pl.when(core == adder)
+        def _():
+            over_all(stage, sent.at[1], count - 2).wait_send()
+            over_all(sums, sent.at[3], total // 2).wait_send()
+
+        @pl.when(core != adder)
+        def _():
+            over_all(stage, sent.at[1], count - 1).wait_send()
+
     over_all(final, peak_r.at[0], count - 1).wait_recv()
 
     high = lax.rem(lax.div(me, SUB), 2) * (WIN // 2)
@@ -468,20 +482,7 @@
             y = jnp.where(lax.div(l_of, rows) == lax.rem(e_of + turn, per_row), y, 0.0)
             out_ref[i:i + 1, to * WIN:(to + 1) * WIN] = jnp.sum(y, axis=0, keepdims=True)
 
-    banks = near + (near - 1) + chips * (cores - 1)
-    over_all(bank_all, sent.at[0], banks).wait_send()
     over_all(final, sent.at[2], count - 1).wait_send()
-    if adder is None:
-        over_all(stage, sent.at[1], count - 1).wait_send()
-    else:
-        @pl.when(core == adder)
-        def _():
-            over_all(stage, sent.at[1], count - 2).wait_send()
-            over_all(sums, sent.at[3], total // 2).wait_send()
-
-        @pl.when(core != adder)
-        def _():
-            over_all(stage, sent.at[1], count - 1).wait_send()
 
 
 def per_device(chips, cores, basis_series, reconstruction, offsets):

time: 29.3 us -> 29.3 us (level)
  no operation moved by 1% of the time
where the time goes in v6:
time: 29.3 us; the launch traced here: 29.1 us
  Pallas kernels  28.5 us (97%)
  local copies, waits for them, and re-layouts  0.6 us (2%)
    pallas_call x1, Pallas kernels, per_device(): pl.pallas_call(functools.partial(kernel, chips, cores, adder), out_shape=...  28.5 us
    unnamed x1, local copies, waits for them, and re-layouts  0.6 us

profile of v6, /device:TPU:0, one launch (start us, length us, event | category | flops | bytes accessed | tf_op | source)
XLA Modules:
  0.0 29.1 jit_solution(9339382031960808703)
XLA Ops:
  0.0 28.5 %shard_map.37 = f32[8,128]{1,0:T(8,128)S(1)} custom-call(s32[3]{0:T(128)} %off_hbm.1, bf16[3,128,1024]{2,1,0:T(8,128)(2,1)} %basis_hbm.1, bf16[3,32,128]{2,1,0:T(8,128)(2,1)} %bitcast.3), custom_call_target="tpu_custom_call" | custom-call | tf_op jit(solution)/shard_map/pallas_call | solution.py:520
  28.5 0.6 %copy.5 = f32[128,8]{0,1:T(8,128)} copy(f32[128,8]{0,1:T(8,128)S(1)} %bitcast.2) | data formatting | bytes 8192

commit v7 on v6

--- a/solution.py
+++ b/solution.py
@@ -275,8 +275,8 @@
         if adder is not None:
             pl.when(core != adder)(near_copy(close(k), core).start)
 
+    over(1, near // 2, lambda k: release(near // 2 - k))
     over(1, near // 2, lambda k: release(near - k))
-    over(1, near // 2, lambda k: release(near // 2 - k))
 
     over(1, near, lambda k: pass_on(across(close(k)) * cores + core))
     load_off.wait()
@@ -383,13 +383,13 @@
 
     pieces(chip, lambda src: bank_copy(chip, src).wait_recv())
     owned = bank_max(bank_all, across(chip) * cores + core)
-    if adder is not None:
-        pl.when(core == adder)(add_near)
-
     pieces(across(chip), lambda src: bank_copy(chip, src).wait_recv())
     powers_for(across(chip), bank_all, across(chip) * cores)
     for d in range(1, cores):
         pow_copy(chip, other_core(d), me).start()
+
+    if adder is not None:
+        pl.when(core == adder)(add_near)
 
     def far_powers(k):
         j = across(close(k))

time: 29.3 us -> 29.3 us (level)
  no operation moved by 1% of the time
where the time goes in v7:
time: 29.3 us; the launch traced here: 29.1 us
  Pallas kernels  28.5 us (97%)
  local copies, waits for them, and re-layouts  0.6 us (2%)
    pallas_call x1, Pallas kernels, per_device(): pl.pallas_call(functools.partial(kernel, chips, cores, adder), out_shape=...  28.5 us
    unnamed x1, local copies, waits for them, and re-layouts  0.6 us

profile of v7, /device:TPU:0, one launch (start us, length us, event | category | flops | bytes accessed | tf_op | source)
XLA Modules:
  0.0 29.1 jit_solution(4637350092953139844)
XLA Ops:
  0.0 28.5 %shard_map.37 = f32[8,128]{1,0:T(8,128)S(1)} custom-call(s32[3]{0:T(128)} %off_hbm.1, bf16[3,128,1024]{2,1,0:T(8,128)(2,1)} %basis_hbm.1, bf16[3,32,128]{2,1,0:T(8,128)(2,1)} %bitcast.3), custom_call_target="tpu_custom_call" | custom-call | tf_op jit(solution)/shard_map/pallas_call | solution.py:520
  28.5 0.6 %copy.5 = f32[128,8]{0,1:T(8,128)} copy(f32[128,8]{0,1:T(8,128)S(1)} %bitcast.2) | data formatting | bytes 8192
